TPU v7x, 128 devices: a whole 4x4x4 slice. The times are simulated.
128 devices in a mesh: dp: 8 (over y, core), mp: 16 (over x, z).
Axes of the slice: x: 4, y: 4, z: 4, core: 2. Of those that a mesh axis runs over, the one named last changes fastest.
Arguments:
- emb_grad: float32 [65536, 7168], P('dp', 'mp'), may hold values from -600 to 600
- mtp_grad: float32 [14336, 7168], P('dp', 'mp'), may hold values from -600 to 600
- emb_groups: int32 [64], replicated, may hold values from 0 to 31
- mtp_groups: int32 [32], replicated, may hold values from 0 to 31
- max_rms: float32 [1], replicated, may hold values from 0.5 to 2
Outputs:
- emb_clipped: bfloat16 [65536, 7168], P(('dp', 'mp'))
- mtp_clipped: bfloat16 [14336, 7168], P('dp', 'mp')
- group_rms: float32 [32], replicated
All inputs are finite; a program needn't handle non-finite values.
Results may differ from a plain program's by a relative error of at most 0.005.
Values may be sent and summed in bfloat16 or wider, within the bound.
No kernel may reach another device: no remote copies, remote signals or barrier semaphores. Data moves between devices by JAX's collectives and lax.ppermute only.
A program may use at most 128 MiB of HBM per device.

v0:
```python
import jax
import jax.numpy as jnp
from jax import lax
from jax.sharding import Mesh
from jax.sharding import PartitionSpec as P

D = 7168
V = 65536
CAT = 14336
EMB_BLK = 1024
MTP_BLK = 448
GROUPS = 32
DP = ("dp_0", "dp_1")
DP_MP = ("dp_0", "dp_1", "mp_0", "mp_1")
MP = ("mp_0", "mp_1")


def one_axis_at_a_time(value, axes):
    for axis in axes:
        value = lax.psum(value, axis)
    return value


def block_squares(gradient, block_rows):
    blocks = gradient.reshape(gradient.shape[0] // block_rows, block_rows, gradient.shape[1])
    return jnp.sum(jnp.square(blocks), axis=(1, 2))


def membership(labels):
    return (labels[:, None] == jnp.arange(GROUPS, dtype=jnp.int32)[None, :]).astype(jnp.float32)


def on_device(emb_grad, mtp_grad, emb_groups, mtp_groups, max_rms):
    shard = lax.axis_index(DP)
    embed_count = emb_grad.shape[0] // EMB_BLK
    head_count = mtp_grad.shape[0] // MTP_BLK
    embed_labels = lax.dynamic_slice_in_dim(emb_groups, shard * embed_count, embed_count)
    head_labels = lax.dynamic_slice_in_dim(mtp_groups, shard * head_count, head_count)
    emb_low = lax.optimization_barrier(emb_grad.astype(jnp.bfloat16))
    partial_value = jnp.sum(
        block_squares(emb_grad, EMB_BLK)[:, None] * membership(embed_labels), axis=0
    )
    partial_value = partial_value + jnp.sum(
        block_squares(mtp_grad, MTP_BLK)[:, None] * membership(head_labels), axis=0
    )
    group_square = one_axis_at_a_time(partial_value, DP_MP)
    group_size = jnp.sum(membership(emb_groups), axis=0) * jnp.float32(EMB_BLK * D) + jnp.sum(
        membership(mtp_groups), axis=0
    ) * jnp.float32(MTP_BLK * D)
    group_rms = jnp.sqrt(group_square / jnp.maximum(group_size, 1.0))
    global_norm = jnp.sqrt(jnp.sum(group_square))
    ceiling = max_rms[0] * jnp.sqrt(jnp.float32((V + CAT) * D))
    factor = ceiling / (global_norm + 1e-06)
    head_output = (mtp_grad * factor).astype(jnp.bfloat16)
    scaled = (emb_low.astype(jnp.float32) * factor).astype(jnp.bfloat16)
    embed_output = lax.all_to_all(scaled, MP, split_axis=0, concat_axis=1, tiled=True)
    return (embed_output, head_output, group_rms)


def solution(mesh):
    torus = Mesh(mesh.devices.reshape(4, 2, 4, 4), ("dp_0", "dp_1", "mp_0", "mp_1"))
    return jax.shard_map(
        on_device,
        mesh=torus,
        in_specs=(P(DP, MP), P(DP, MP), P(), P(), P()),
        out_specs=(P(DP_MP, None), P(DP, MP), P()),
        check_vma=False,
    )
```

profile of v0, /device:TPU:0, one launch (start us, length us, event | category | flops | bytes accessed | tf_op | source)
XLA Modules:
  0.0 171.9 jit_solution(9425515222135174412)
XLA Ops:
  1.3 0.8 convert_reduce_fusion.1
  2.0 0.7 dynamic_slice.6
  2.8 0.7 convert_reduce_fusion
  3.5 0.7 dynamic_slice.7
  4.3 2.2 %multiply_reduce_fusion.1 = f32[1792]{0:T(1024)S(1)} fusion(f32[1792,448]{0,1:T(8,128)} %param.6), kind=kLoop, calls=%fused_computation.4 | loop fusion | flops 1603840 | bytes 3218432 | tf_op jit(solution)/shard_map/reduce_sum | solution.py:26
  6.4 0.1 reduce_sum.82
  6.5 14.2 %multiply_reduce_fusion = (f32[8192]{0:T(1024)S(1)}, bf16[8192,448]{0,1:T(8,128)(2,1)}) fusion(f32[8192,448]{0,1:T(8,128)} %param.5), kind=kLoop, calls=%fused_computation.1 | loop fusion | flops 11001856 | bytes 22052864 | tf_op jit(solution)/shard_map/reduce_sum | solution.py:26
  20.7 0.1 reduce_sum.83
  20.8 0.1 reduce_sum.79
  20.9 0.1 select_reduce_fusion.1
  21.0 0.1 select_reduce_fusion
  21.1 10.9 %psum.28 = f32[32]{0:T(128)S(1)} all-reduce(f32[32]{0:T(128)S(1)} %add.29), channel_id=1, replica_groups=mesh['dp_0'=4,'dp_1'=2,'mp_0'=4,'mp_1'=4] {'dp_0'}, use_global_device_ids=true, to_apply=%region_6.0 | all-reduce | flops 32 | bytes 256 | tf_op jit(solution)/shard_map/psum | solution.py:20
  32.0 2.5 %psum.29 = f32[32]{0:T(128)S(1)} all-reduce(f32[32]{0:T(128)S(1)} %psum.28), channel_id=1, replica_groups=mesh['dp_0'=4,'dp_1'=2,'mp_0'=4,'mp_1'=4] {'dp_1'}, use_global_device_ids=true, to_apply=%region_7.0 | all-reduce | flops 32 | bytes 256 | tf_op jit(solution)/shard_map/psum | solution.py:20
  34.4 10.5 %psum.30 = f32[32]{0:T(128)S(1)} all-reduce(f32[32]{0:T(128)S(1)} %psum.29), channel_id=1, replica_groups=mesh['dp_0'=4,'dp_1'=2,'mp_0'=4,'mp_1'=4] {'mp_0'}, use_global_device_ids=true, to_apply=%region_8.0 | all-reduce | flops 32 | bytes 256 | tf_op jit(solution)/shard_map/psum | solution.py:20
  44.9 11.8 %psum.31 = f32[32]{0:T(128)S(1)} all-reduce(f32[32]{0:T(128)S(1)} %psum.30), channel_id=1, replica_groups=mesh['dp_0'=4,'dp_1'=2,'mp_0'=4,'mp_1'=4] {'mp_1'}, use_global_device_ids=true, to_apply=%region_9.0 | all-reduce | flops 32 | bytes 256 | tf_op jit(solution)/shard_map/psum | solution.py:20
  56.6 1.1 fusion
  58.5 4.9 %multiply_convert_fusion = bf16[8192,448]{0,1:T(8,128)(2,1)S(1)} fusion(bf16[8192,448]{0,1:T(8,128)(2,1)} %get-tuple-element.16, f32[]{:T(128)S(6)} %div.6), kind=kLoop, calls=%fused_computation | loop fusion | flops 11010048 | bytes 14680068 | tf_op jit(solution)/shard_map/convert_element_type | solution.py:55
  63.4 3.9 %copy.18 = bf16[56,16,8,512]{3,2,0,1:T(8,128)(2,1)} copy(bf16[56,16,8,512]{3,2,1,0:T(8,128)(2,1)S(1)} %bitcast.9) | data formatting | bytes 14680064 | tf_op jit(solution)/shard_map/all_to_all | solution.py:56
  67.2 0.0 copy-start
  67.2 5.0 %all-to-all-start = ((bf16[16,512,448]{1,2,0:T(8,128)(2,1)}), bf16[16,512,448]{1,2,0:T(8,128)(2,1)}, u32[]{:S(2)}, u32[]{:S(2)}) async-start(bf16[16,512,448]{1,2,0:T(8,128)(2,1)} %bitcast.8), calls=%async_computation | async-start | bytes 14680064 | tf_op jit(solution)/shard_map/all_to_all | solution.py:56
  72.2 0.0 copy-done
  72.2 1.4 multiply_convert_fusion.1
  73.6 88.4 %all-to-all-done = bf16[16,512,448]{1,2,0:T(8,128)(2,1)} async-done(((bf16[16,512,448]{1,2,0:T(8,128)(2,1)}), bf16[16,512,448]{1,2,0:T(8,128)(2,1)}, u32[]{:S(2)}, u32[]{:S(2)}) %all-to-all-start) | async-done | bytes 7340064 | tf_op jit(solution)/shard_map/all_to_all | solution.py:56
  162.0 9.9 %copy.15 = bf16[512,7168]{1,0:T(8,128)(2,1)} copy(bf16[512,7168]{0,1:T(8,128)(2,1)} %bitcast.2) | data formatting | bytes 14680064
  (2 shorter events, 0.0 us)
Async XLA Ops:
  67.2 5.0 %copy-start = (f32[1792,448]{0,1:T(8,128)S(1)}, f32[1792,448]{0,1:T(8,128)}, u32[]{:S(2)}) copy-start(f32[1792,448]{0,1:T(8,128)} %param.6) | copy-start | bytes 9633796
  67.2 94.8 %all-to-all-start = ((bf16[16,512,448]{1,2,0:T(8,128)(2,1)}), bf16[16,512,448]{1,2,0:T(8,128)(2,1)}, u32[]{:S(2)}, u32[]{:S(2)}) async-start(bf16[16,512,448]{1,2,0:T(8,128)(2,1)} %bitcast.8), calls=%async_computation | async-start | bytes 14680064 | tf_op jit(solution)/shard_map/all_to_all | solution.py:56
where the time goes:
time: 173 us; the launch traced here: 172 us
  waiting for transfers between devices  88.4 us (51%)
  blocking collectives  35.5 us (21%)
  other arithmetic  25.6 us (15%)
  local copies, waits for them, and re-layouts  15.3 us (9%)
  starting transfers between devices  4.95 us (3%)
  between operations  2.06 us (1%)
    all_to_all x1, waiting for transfers between devices, on_device(): lax.all_to_all(scaled, MP, split_axis=0, concat_axis=1, tiled=True)  88.4 us
    psum x4, blocking collectives, one_axis_at_a_time(): value = lax.psum(value, axis)  35.5 us
    reduce_sum x4, other arithmetic, block_squares(): return jnp.sum(jnp.square(blocks), axis=(1, 2))  16.6 us
    unnamed x3, local copies, waits for them, and re-layouts  9.94 us
    all_to_all x1, starting transfers between devices, on_device(): lax.all_to_all(scaled, MP, split_axis=0, concat_axis=1, tiled=True)  4.95 us
    convert_element_type x1, other arithmetic, on_device(): scaled = (emb_low.astype(jnp.float32) * factor).astype(jnp.bfloat16)  4.88 us
    all_to_all x1, local copies, waits for them, and re-layouts, on_device(): lax.all_to_all(scaled, MP, split_axis=0, concat_axis=1, tiled=True)  3.85 us
  transfers between devices with their start and end apart: 1, of which 1 were waited for; matrix products, arithmetic and copies ran while one was open for 1% of the time, Pallas kernels for 0%

commit v1 on v0

v1 whole, which is shorter than its diff:
```python
import jax
import jax.numpy as jnp
from jax import lax
from jax.experimental import pallas as pl
from jax.experimental.pallas import tpu as pltpu
from jax.sharding import Mesh
from jax.sharding import PartitionSpec as P

D = 7168
V = 65536
CAT = 14336
EMB_BLK = 1024
MTP_BLK = 448
GROUPS = 32
DP = ("dp_0", "dp_1")
DP_MP = ("dp_0", "dp_1", "mp_0", "mp_1")
MP = ("mp_0", "mp_1")
PEERS = 16
FEAT = 448
OWN = 512
EXTRA = 16
F32 = jnp.float32
BF16 = jnp.bfloat16
VMEM_LIMIT = 48 * 1024 * 1024


def membership(labels):
    return (labels[:, None] == jnp.arange(GROUPS, dtype=jnp.int32)[None, :]).astype(F32)


def fold_squares(x):
    s = x * x
    t = jnp.sum(s.reshape(FEAT // 8, 8, s.shape[1]), axis=0)
    r = t[:, :128]
    for i in range(1, s.shape[1] // 128):
        r = r + t[:, 128 * i : 128 * (i + 1)]
    return r


def first_kernel(x_ref, piece_ref, acc_ref):
    x = x_ref[...]
    piece_ref[0] = x.astype(BF16)
    acc_ref[0] = fold_squares(x)


def first_pass(grad_t, rows):
    return pl.pallas_call(
        first_kernel,
        grid=(PEERS,),
        in_specs=[pl.BlockSpec((FEAT, rows), lambda p: (0, p * (OWN // rows)))],
        out_specs=[
            pl.BlockSpec((1, FEAT, rows), lambda p: (p, 0, 0)),
            pl.BlockSpec((1, 8, 128), lambda p: (p, 0, 0)),
        ],
        out_shape=[
            jax.ShapeDtypeStruct((PEERS, FEAT, rows), BF16),
            jax.ShapeDtypeStruct((PEERS, 8, 128), F32),
        ],
        compiler_params=pltpu.CompilerParams(vmem_limit_bytes=VMEM_LIMIT),
        name="first_pass",
    )(grad_t)


def second_kernel(labels_ref, xa_ref, xb_ref, m_ref, acc0_ref, mid_ref, last_ref, acc_ref, macc_ref):
    p = pl.program_id(0)
    xa = xa_ref[...]
    xb = xb_ref[...]
    mid_ref[p, :FEAT, :] = xa.astype(BF16)
    last_ref[0] = xb.astype(BF16)
    acc_ref[p] = acc0_ref[0] + fold_squares(xa) + fold_squares(xb)

    @pl.when(p == 0)
    def _():
        macc_ref[...] = jnp.zeros_like(macc_ref)

    @pl.when(p % 2 == 0)
    def _():
        m = m_ref[...]
        macc_ref[...] += jnp.sum((m * m).reshape(m.shape[0] // 8, 8, m.shape[1]), axis=0)

    @pl.when(p == PEERS - 1)
    def _():
        lane = lax.broadcasted_iota(jnp.int32, (8, 128), 1)
        total = jnp.zeros((8, 128), F32)
        for b in range(PEERS // 2):
            s = jnp.sum(acc_ref[2 * b] + acc_ref[2 * b + 1])
            total = total + jnp.where(lane == labels_ref[b], s, 0.0)
        col = lax.broadcasted_iota(jnp.int32, macc_ref.shape, 1)
        for b in range(4):
            s = jnp.sum(jnp.where((col >= MTP_BLK * b) & (col < MTP_BLK * (b + 1)), macc_ref[...], 0.0))
            total = total + jnp.where(lane == labels_ref[8 + b], s, 0.0)
        high = total.astype(BF16).astype(F32)
        middle = (total - high).astype(BF16).astype(F32)
        low = total - high - middle
        row = lax.broadcasted_iota(jnp.int32, (8, 128), 0)
        parts = jnp.where(row == 0, high, jnp.where(row == 1, middle, jnp.where(row == 2, low, 0.0)))
        parts = jnp.concatenate([parts, jnp.zeros((8, 128), F32)], axis=0).astype(BF16)
        for q in range(PEERS):
            mid_ref[q, FEAT:, :] = parts


def second_pass(grad_t, mtp_t, labels, acc0):
    return pl.pallas_call(
        second_kernel,
        grid_spec=pltpu.PrefetchScalarGridSpec(
            num_scalar_prefetch=1,
            grid=(PEERS,),
            in_specs=[
                pl.BlockSpec((FEAT, 128), lambda p, l: (0, 4 * p + 1)),
                pl.BlockSpec((FEAT, 256), lambda p, l: (0, 2 * p + 1)),
                pl.BlockSpec((56, 1792), lambda p, l: (p // 2, 0)),
                pl.BlockSpec((1, 8, 128), lambda p, l: (p, 0, 0)),
            ],
            out_specs=[
                pl.BlockSpec((PEERS, FEAT + EXTRA, 128), lambda p, l: (0, 0, 0)),
                pl.BlockSpec((1, FEAT, 256), lambda p, l: (p, 0, 0)),
            ],
            scratch_shapes=[pltpu.VMEM((PEERS, 8, 128), F32), pltpu.VMEM((8, 1792), F32)],
        ),
        out_shape=[
            jax.ShapeDtypeStruct((PEERS, FEAT + EXTRA, 128), BF16),
            jax.ShapeDtypeStruct((PEERS, FEAT, 256), BF16),
        ],
        compiler_params=pltpu.CompilerParams(vmem_limit_bytes=VMEM_LIMIT),
        name="second_pass",
    )(labels, grad_t, grad_t, mtp_t, acc0)


def place_kernel(factor_ref, x_ref, *rest):
    out_ref = rest[-1]
    x = x_ref[:, :FEAT, :].astype(F32)
    out_ref[...] = (x.reshape(2 * FEAT, x.shape[2]).T * factor_ref[0]).astype(BF16)


def place(factor, received, base, start):
    peers, feat, rows = received.shape
    specs = [
        pl.BlockSpec(memory_space=pltpu.SMEM),
        pl.BlockSpec((2, feat, rows), lambda j: (j, 0, 0)),
    ]
    args = [factor, received]
    alias = {}
    if base is not None:
        specs.append(pl.BlockSpec(memory_space=pl.ANY))
        args.append(base)
        alias = {2: 0}
    return pl.pallas_call(
        place_kernel,
        grid=(PEERS // 2,),
        in_specs=specs,
        out_specs=pl.BlockSpec((rows, 2 * FEAT), lambda j: (start // rows, j)),
        out_shape=jax.ShapeDtypeStruct((OWN, D), BF16),
        input_output_aliases=alias,
        compiler_params=pltpu.CompilerParams(vmem_limit_bytes=VMEM_LIMIT),
        name="place",
    )(*args)


def exchange(pieces):
    return lax.all_to_all(pieces, MP, split_axis=0, concat_axis=0, tiled=True)


def on_device(emb_grad, mtp_grad, emb_groups, mtp_groups, max_rms):
    shard = lax.axis_index(DP)
    labels = jnp.concatenate(
        [
            lax.dynamic_slice_in_dim(emb_groups, shard * 8, 8),
            lax.dynamic_slice_in_dim(mtp_groups, shard * 4, 4),
        ]
    )
    grad_t = emb_grad.T
    mtp_t = mtp_grad.T
    p0, acc0 = first_pass(grad_t, 128)
    r0 = exchange(p0)
    p1, p2 = second_pass(grad_t, mtp_t, labels, acc0)
    r1 = exchange(p1)
    r2 = exchange(p2)
    group_square = jnp.sum(r1[:, FEAT : FEAT + 3, :GROUPS].astype(F32), axis=(0, 1))
    for axis in DP:
        group_square = lax.psum(group_square, axis)
    group_size = jnp.sum(membership(emb_groups), axis=0) * F32(EMB_BLK * D) + jnp.sum(
        membership(mtp_groups), axis=0
    ) * F32(MTP_BLK * D)
    group_rms = jnp.sqrt(group_square / jnp.maximum(group_size, 1.0))
    global_norm = jnp.sqrt(jnp.sum(group_square))
    ceiling = max_rms[0] * jnp.sqrt(F32((V + CAT) * D))
    factor = ceiling / (global_norm + 1e-06)
    head_output = (mtp_grad * factor).astype(BF16)
    scale = factor.reshape(1)
    out = place(scale, r0, None, 0)
    out = place(scale, r1, out, 128)
    out = place(scale, r2, out, 256)
    return (out, head_output, group_rms)


def solution(mesh):
    torus = Mesh(mesh.devices.reshape(4, 2, 4, 4), ("dp_0", "dp_1", "mp_0", "mp_1"))
    return jax.shard_map(
        on_device,
        mesh=torus,
        in_specs=(P(DP, MP), P(DP, MP), P(), P(), P()),
        out_specs=(P(DP_MP, None), P(DP, MP), P()),
        check_vma=False,
    )
```

time: 173 us -> 129 us (0.75)
  waiting for transfers between devices: 88.4 us -> 28.2 us
  Pallas kernels: 0 us -> 37.7 us
  other arithmetic: 25.6 us -> 3.56 us
  local copies, waits for them, and re-layouts: 15.3 us -> 2.66 us
  starting transfers between devices: 4.95 us -> 12.8 us
  blocking collectives: 35.5 us -> 41.2 us
    all_to_all x1 -> x2, waiting for transfers between devices: 88.4 us -> 28.2 us  [exchange(): return lax.all_to_all(pieces, MP, split_axis=0, concat_axis=0, tiled=True)]
    pallas_call x0 -> x5, Pallas kernels: none -> 37.7 us  [the longest x3 16.6 us: place(): pl.pallas_call(place_kernel, grid=(PEERS // 2,), in_specs=specs, out_spec...]
    all_to_all x0 -> x1, blocking collectives: none -> 28 us  [exchange(): return lax.all_to_all(pieces, MP, split_axis=0, concat_axis=0, tiled=True)]
    psum x4 -> x2, blocking collectives: 35.5 us -> 13.2 us  [on_device(): group_square = lax.psum(group_square, axis)]
    reduce_sum x8 -> x3, other arithmetic: 18.3 us -> 1 us  [the longest x1 0.8 us: on_device(): jnp.sum(r1[:, FEAT:FEAT + 3, :GROUPS].astype(F32), axis=(0, 1))]
    all_to_all x1 -> x2, starting transfers between devices: 4.95 us -> 12.8 us  [exchange(): return lax.all_to_all(pieces, MP, split_axis=0, concat_axis=0, tiled=True)]
    unnamed x3 -> x12, local copies, waits for them, and re-layouts: 9.94 us -> 2.51 us
    convert_element_type x2 -> x1, other arithmetic: 6.24 us -> 1.35 us  [on_device(): head_output = (mtp_grad * factor).astype(BF16)]
  transfers between devices with their start and end apart: 1 -> 2, of which waited for: 1 -> 2; matrix products, arithmetic and copies ran while one was open for 1% -> 3% of each run, Pallas kernels for 0% -> 17%
where the time goes in v1:
time: 129 us; the launch traced here: 128 us
  blocking collectives  41.2 us (32%)
  Pallas kernels  37.7 us (29%)
  waiting for transfers between devices  28.2 us (22%)
  starting transfers between devices  12.8 us (10%)
  other arithmetic  3.56 us (3%)
  local copies, waits for them, and re-layouts  2.66 us (2%)
  between operations  2.08 us (2%)
    all_to_all x2, waiting for transfers between devices, exchange(): return lax.all_to_all(pieces, MP, split_axis=0, concat_axis=0, tiled=True)  28.2 us
    all_to_all x1, blocking collectives, exchange(): return lax.all_to_all(pieces, MP, split_axis=0, concat_axis=0, tiled=True)  28 us
    pallas_call x3, Pallas kernels, place(): pl.pallas_call(place_kernel, grid=(PEERS // 2,), in_specs=specs, out_spec...  16.6 us
    psum x2, blocking collectives, on_device(): group_square = lax.psum(group_square, axis)  13.2 us
    all_to_all x2, starting transfers between devices, exchange(): return lax.all_to_all(pieces, MP, split_axis=0, concat_axis=0, tiled=True)  12.8 us
    pallas_call x1, Pallas kernels, second_pass(): pl.pallas_call(second_kernel, grid_spec=pltpu.PrefetchScalarGridSpec(num_...  12.8 us
    pallas_call x1, Pallas kernels, first_pass(): pl.pallas_call(first_kernel, grid=(PEERS,), in_specs=[pl.BlockSpec((FEAT,...  8.3 us
  transfers between devices with their start and end apart: 2, of which 2 were waited for; matrix products, arithmetic and copies ran while one was open for 3% of the time, Pallas kernels for 17%

profile of v1, /device:TPU:0, one launch (start us, length us, event | category | flops | bytes accessed | tf_op | source)
XLA Modules:
  0.0 128.2 jit_solution(17634392092657685701)
XLA Ops:
  0.6 8.3 %first_pass.1 = (bf16[16,448,128]{2,1,0:T(8,128)(2,1)S(1)}, f32[16,8,128]{2,1,0:T(8,128)S(1)}) custom-call(f32[448,8192]{1,0:T(8,128)} %bitcast.5), custom_call_target="tpu_custom_call" | custom-call | tf_op jit(solution)/shard_map/first_pass/pallas_call | solution.py:47
  8.9 0.0 copy-start.3
  8.9 1.2 copy-done.3
  10.2 0.0 copy-start.5
  10.2 0.0 copy-start.4
  10.2 0.0 copy-start
  10.2 8.3 %all-to-all-start.2 = ((bf16[16,448,128]{2,1,0:T(8,128)(2,1)}), bf16[16,448,128]{2,1,0:T(8,128)(2,1)}, u32[]{:S(2)}, u32[]{:S(2)}) async-start(bf16[16,448,128]{2,1,0:T(8,128)(2,1)} %copy-done.3), calls=%async_computation.2 | async-start | bytes 3670016 | tf_op jit(solution)/shard_map/all_to_all | solution.py:160
  18.5 0.0 copy-done.5
  18.5 0.1 dynamic_slice.7
  18.6 0.0 copy-done.4
  18.6 0.1 dynamic_slice.6
  18.7 0.1 pad_add_fusion.labels_ref
  18.7 0.0 copy-done
  18.8 12.8 %second_pass.1 = (bf16[16,464,128]{2,1,0:T(8,128)(2,1)S(1)}, bf16[16,448,256]{2,1,0:T(8,128)(2,1)}) custom-call(s32[12]{0:T(128)S(1)} %pad_add_fusion.labels_ref, f32[448,8192]{1,0:T(8,128)} %bitcast.6, f32[448,8192]{1,0:T(8,128)} %bitcast.7, f32[448,1792]{1,0:T(8,128)S(1)} %bitcast.4, f32[16,8,128]{2,1,0:T(8,128)S(1)} %get-tuple-element.7.acc0_ref), custom_call_target="tpu_custom_call" | custom-call | tf_op jit(solution)/shard_map/second_pass/pallas_call | solution.py:103
  31.5 0.0 copy-start.2
  31.5 1.2 copy-done.2
  32.8 12.9 %all-to-all-done.2.x_ref = bf16[16,448,128]{2,1,0:T(8,128)(2,1)} async-done(((bf16[16,448,128]{2,1,0:T(8,128)(2,1)}), bf16[16,448,128]{2,1,0:T(8,128)(2,1)}, u32[]{:S(2)}, u32[]{:S(2)}) %all-to-all-start.2) | async-done | bytes 1835040 | tf_op jit(solution)/shard_map/all_to_all | solution.py:160
  45.7 28.0 %all_to_all.15.x_ref = bf16[16,464,128]{2,1,0:T(8,128)(2,1)} all-to-all(bf16[16,464,128]{2,1,0:T(8,128)(2,1)} %copy-done.2), channel_id=1, replica_groups=mesh['dp_0'=4,'dp_1'=2,'mp_0'=4,'mp_1'=4] {'mp_0','mp_1'}, dimensions={0} | all-to-all | bytes 3801088 | tf_op jit(solution)/shard_map/all_to_all | solution.py:160
  73.7 4.5 %all-to-all-start.1 = ((bf16[16,448,256]{2,1,0:T(8,128)(2,1)}), bf16[16,448,256]{2,1,0:T(8,128)(2,1)}, u32[]{:S(2)}, u32[]{:S(2)}) async-start(bf16[16,448,256]{2,1,0:T(8,128)(2,1)} %get-tuple-element.9), calls=%async_computation.1 | async-start | bytes 7340032 | tf_op jit(solution)/shard_map/all_to_all | solution.py:160
  78.9 0.1 convert_reduce_fusion.2
  79.0 0.1 convert_reduce_fusion.1
  79.1 0.8 convert_reduce_fusion
  79.9 10.7 %psum.14 = f32[32]{0:T(128)S(1)} all-reduce(f32[32]{0:T(128)S(1)} %convert_reduce_fusion), channel_id=1, replica_groups=mesh['dp_0'=4,'dp_1'=2,'mp_0'=4,'mp_1'=4] {'dp_0'}, use_global_device_ids=true, to_apply=%region_1.0 | all-reduce | flops 32 | bytes 256 | tf_op jit(solution)/shard_map/psum | solution.py:180
  90.6 2.5 %psum.15 = f32[32]{0:T(128)S(1)} all-reduce(f32[32]{0:T(128)S(1)} %psum.14), channel_id=1, replica_groups=mesh['dp_0'=4,'dp_1'=2,'mp_0'=4,'mp_1'=4] {'dp_1'}, use_global_device_ids=true, to_apply=%region_2.0 | all-reduce | flops 32 | bytes 256 | tf_op jit(solution)/shard_map/psum | solution.py:180
  93.0 1.1 fusion
  94.9 0.0 copy-start.1
  94.9 6.1 %place.3.rest_0_ = bf16[512,7168]{1,0:T(8,128)(2,1)} custom-call(f32[1]{0:T(128)} %bitcast.3.factor_ref, bf16[16,448,128]{2,1,0:T(8,128)(2,1)} %all-to-all-done.2.x_ref), custom_call_target="tpu_custom_call" | custom-call | tf_op jit(solution)/shard_map/place/pallas_call | solution.py:147
  101.1 0.0 copy-done.1
  101.1 3.5 %place.4.rest_0_ = bf16[512,7168]{1,0:T(8,128)(2,1)} custom-call(f32[1]{0:T(128)} %bitcast.3.factor_ref, bf16[16,464,128]{2,1,0:T(8,128)(2,1)S(1)} %copy-done.1, bf16[512,7168]{1,0:T(8,128)(2,1)} %place.3.rest_0_), custom_call_target="tpu_custom_call", output_to_operand_aliasing={{}: (2, {})} | custom-call | tf_op jit(solution)/shard_map/place/pallas_call | solution.py:147
  104.5 1.4 %multiply_convert_fusion = bf16[1792,448]{0,1:T(8,128)(2,1)} fusion(f32[1792,448]{0,1:T(8,128)S(1)} %copy-done, f32[]{:T(128)} %div.6), kind=kLoop, calls=%fused_computation | loop fusion | flops 1605632 | bytes 4816900 | tf_op jit(solution)/shard_map/convert_element_type | solution.py:188
  105.9 15.4 %all-to-all-done.1.x_ref = bf16[16,448,256]{2,1,0:T(8,128)(2,1)} async-done(((bf16[16,448,256]{2,1,0:T(8,128)(2,1)}), bf16[16,448,256]{2,1,0:T(8,128)(2,1)}, u32[]{:S(2)}, u32[]{:S(2)}) %all-to-all-start.1) | async-done | bytes 3670048 | tf_op jit(solution)/shard_map/all_to_all | solution.py:160
  121.2 7.0 %place.5 = bf16[512,7168]{1,0:T(8,128)(2,1)} custom-call(f32[1]{0:T(128)} %bitcast.3.factor_ref, bf16[16,448,256]{2,1,0:T(8,128)(2,1)} %all-to-all-done.1.x_ref, bf16[512,7168]{1,0:T(8,128)(2,1)} %place.4.rest_0_), custom_call_target="tpu_custom_call", output_to_operand_aliasing={{}: (2, {})} | custom-call | tf_op jit(solution)/shard_map/place/pallas_call | solution.py:147
Async XLA Ops:
  8.9 1.3 copy-start.3
  10.2 8.3 %copy-start.5 = (s32[32]{0:T(128)S(1)}, s32[32]{0:T(128)}, u32[]{:S(2)}) copy-start(s32[32]{0:T(128)} %param.8) | copy-start | bytes 388
  10.2 8.4 %copy-start.4 = (s32[64]{0:T(128)S(1)}, s32[64]{0:T(128)}, u32[]{:S(2)}) copy-start(s32[64]{0:T(128)} %param.7) | copy-start | bytes 772
  10.2 8.6 %copy-start = (f32[1792,448]{0,1:T(8,128)S(1)}, f32[1792,448]{0,1:T(8,128)}, u32[]{:S(2)}) copy-start(f32[1792,448]{0,1:T(8,128)} %param.6) | copy-start | bytes 9633796
  10.2 35.5 %all-to-all-start.2 = ((bf16[16,448,128]{2,1,0:T(8,128)(2,1)}), bf16[16,448,128]{2,1,0:T(8,128)(2,1)}, u32[]{:S(2)}, u32[]{:S(2)}) async-start(bf16[16,448,128]{2,1,0:T(8,128)(2,1)} %copy-done.3), calls=%async_computation.2 | async-start | bytes 3670016 | tf_op jit(solution)/shard_map/all_to_all | solution.py:160
  31.5 1.2 copy-start.2
  73.7 47.5 %all-to-all-start.1 = ((bf16[16,448,256]{2,1,0:T(8,128)(2,1)}), bf16[16,448,256]{2,1,0:T(8,128)(2,1)}, u32[]{:S(2)}, u32[]{:S(2)}) async-start(bf16[16,448,256]{2,1,0:T(8,128)(2,1)} %get-tuple-element.9), calls=%async_computation.1 | async-start | bytes 7340032 | tf_op jit(solution)/shard_map/all_to_all | solution.py:160
  94.9 6.2 %copy-start.1 = (bf16[16,464,128]{2,1,0:T(8,128)(2,1)S(1)}, bf16[16,464,128]{2,1,0:T(8,128)(2,1)}, u32[]{:S(2)}) copy-start(bf16[16,464,128]{2,1,0:T(8,128)(2,1)} %all_to_all.15.x_ref) | copy-start | bytes 5701636
